TPU v7x, 32 devices: a whole 2x2x4 slice. The times are simulated.
32 devices in a mesh: row: 4 (over z), col: 8 (over y, x, core).
Axes of the slice: x: 2, y: 2, z: 4, core: 2. Of those that a mesh axis runs over, the one named last changes fastest.
Arguments:
- factor_wide: float32 [4, 4, 2, 8, 512, 512], P(None, 'row', None, 'col'), may hold values from -1 to 2, as said below
- factor_narrow: bfloat16 [4, 4, 2, 8, 512, 512], P(None, 'row', None, 'col'), may hold values from -1 to 2, as said below
- flags: int32 [4, 4, 2, 8], P(None, 'row', None, 'col'), may hold values from 0 to 1
- forward_solution: float32 [2, 8, 512, 128], P(None, 'col'), may hold values from -0.5 to 0.5
- solution_grad: float32 [2, 8, 512, 128], P(None, 'col'), may hold values from -1.8 to 1.8
Outputs:
- rhs_grad: float32 [4, 4, 512, 128], P(None, 'row')
- factor_grad: float32 [4, 4, 2, 8, 512, 512], P(None, 'row', None, 'col')
Inputs may be any that keep to these rules, and one draw needn't show every extreme that they name: `factor_wide`: the diagonal entries of every diagonal tile lie between 1 and 2. `factor_narrow`: the diagonal entries of every diagonal tile lie between 1 and 2.
All inputs are finite; a program needn't handle non-finite values.
Results may differ from a plain program's by a relative error of at most 0.0003.
Values sent between devices are 32-bit elements; how exact they have to be, the bound alone decides.
A program may use at most 64 MiB of HBM per device.

v0:
```python
import jax
import jax.numpy as jnp
from jax import lax
from jax.sharding import PartitionSpec as P

HIGHEST_PRECISION = lax.Precision.HIGHEST


def broadcast(value, axis, root):
    mine = lax.axis_index(axis) == root
    return lax.psum(jnp.where(mine, value, jnp.zeros_like(value)), axis)


def from_behind(value, axis, by):
    size = lax.axis_size(axis)
    return lax.ppermute(value, axis, [(i, (i + by) % size) for i in range(size)])


def lower_mask(row_index, col_index, tile_width):
    inner_mask = lax.broadcasted_iota(
        jnp.int32, (tile_width, tile_width), 0
    ) >= lax.broadcasted_iota(jnp.int32, (tile_width, tile_width), 1)
    return (row_index > col_index) | (row_index == col_index) & inner_mask


def body(factor_wide, factor_narrow, flags, forward_solution, solution_grad):
    row_count = lax.axis_size("row")
    col_count = lax.axis_size("col")
    my_row = lax.axis_index("row")
    my_col = lax.axis_index("col")
    local_rows = factor_wide.shape[0]
    local_cols = factor_wide.shape[2]
    tile_width = factor_wide.shape[4]
    rhs_width = forward_solution.shape[3]
    tile_count = local_rows * row_count
    factor_tiles = jnp.where(
        flags[:, 0, :, 0, None, None] == 1,
        factor_narrow[:, 0, :, 0].astype(jnp.float32),
        factor_wide[:, 0, :, 0],
    )
    solution_local = forward_solution[:, 0]
    target_local = solution_grad[:, 0]
    row_index = jnp.arange(local_rows, dtype=jnp.int32) * row_count + my_row
    col_index = jnp.arange(local_cols, dtype=jnp.int32) * col_count + my_col
    empty_block = jnp.zeros((tile_width, rhs_width), jnp.float32)

    def nothing_block():
        return empty_block

    def column_partial(rhs_local, target, lowest):

        def on_owner():
            column = lax.dynamic_index_in_dim(factor_tiles, target // col_count, 1, keepdims=False)
            weight = (row_index >= lowest).astype(jnp.float32)
            masked = rhs_local * weight[:, None, None]
            return jnp.einsum("aki,akr->ir", column, masked, precision=HIGHEST_PRECISION)

        return lax.cond(my_col == target % col_count, on_owner, nothing_block)

    def target_block(target):
        return lax.dynamic_index_in_dim(target_local, target // col_count, 0, keepdims=False)

    def advance(right_side, target, carried):
        rhs_local, factor_grad = carried
        local_slot = target // row_count
        holds_row = my_row == target % row_count
        is_owner = holds_row & (my_col == target % col_count)

        def solve_here():
            tile_row = lax.dynamic_index_in_dim(factor_tiles, local_slot, 0, keepdims=False)
            diagonal = lax.dynamic_index_in_dim(tile_row, target // col_count, 0, keepdims=False)
            return lax.linalg.triangular_solve(
                diagonal, right_side, left_side=True, lower=True, transpose_a=True
            )

        solved = lax.cond(is_owner, solve_here, nothing_block)
        arrived = broadcast(solved, "col", target % col_count)
        current = lax.dynamic_index_in_dim(rhs_local, local_slot, 0, keepdims=False)
        rhs_local = lax.dynamic_update_index_in_dim(
            rhs_local, jnp.where(holds_row, arrived, current), local_slot, 0
        )
        return (rhs_local, factor_grad)

    final_index = tile_count - 1
    carried = (
        jnp.zeros((local_rows, tile_width, rhs_width), jnp.float32),
        jnp.zeros((local_rows, local_cols, tile_width, tile_width), jnp.float32),
    )
    carried = advance(target_block(jnp.int32(final_index)), jnp.int32(final_index), carried)

    def sweep_step(offset, loop_state):
        carried, early_sum = loop_state
        target = final_index - 1 - offset
        rhs_local = carried[0]
        source = target + 1

        def compute_fresh():
            tile_row = lax.dynamic_index_in_dim(
                factor_tiles, source // row_count, 0, keepdims=False
            )
            tile_now = lax.dynamic_index_in_dim(tile_row, target // col_count, 0, keepdims=False)
            newest = lax.dynamic_index_in_dim(rhs_local, source // row_count, 0, keepdims=False)
            return jnp.dot(
                tile_now.T, newest, precision=HIGHEST_PRECISION, preferred_element_type=jnp.float32
            )

        fresh_owner = (my_row == source % row_count) & (my_col == target % col_count)
        fresh_term = lax.cond(fresh_owner, compute_fresh, nothing_block)
        moved_term = from_behind(fresh_term, "row", -1)
        following = jnp.maximum(target - 1, 0)
        next_partial = column_partial(rhs_local, following, source)
        next_sum = lax.psum(next_partial, "row")
        carried = advance(target_block(target) - early_sum - moved_term, target, carried)
        return (carried, next_sum)

    carried, unused_sum = lax.fori_loop(0, final_index, sweep_step, (carried, empty_block))
    rhs_local, factor_grad = carried
    products = -jnp.einsum("akr,blr->abkl", rhs_local, solution_local, precision=HIGHEST_PRECISION)
    masks = lower_mask(row_index[:, None, None, None], col_index[None, :, None, None], tile_width)
    factor_grad = jnp.where(masks, products, jnp.zeros_like(products))
    return (rhs_local[:, None], factor_grad[:, None, :, None])


def solution(mesh):
    placed = (
        P(None, "row", None, "col", None, None),
        P(None, "row", None, "col", None, None),
        P(None, "row", None, "col"),
        P(None, "col", None, None),
        P(None, "col", None, None),
    )
    return jax.shard_map(
        body,
        mesh=mesh,
        in_specs=placed,
        out_specs=(P(None, "row", None, None), P(None, "row", None, "col", None, None)),
        check_vma=False,
    )
```

profile of v0, /device:TPU:0, one launch (start us, length us, event | category | flops | bytes accessed | tf_op | source)
XLA Modules:
  0.0 2219.2 jit_solution(8826648313586827079)
XLA Ops:
  7.3 9.9 copy.12
  17.2 7.3 copy.11
  24.5 9.6 convert_select_fusion
  35.9 117.2 %all-reduce.5.cloned.1.call-done = f32[512,128]{1,0:T(8,128)} async-done(((f32[512,128]{1,0:T(8,128)}), f32[512,128]{1,0:T(8,128)}) %all-reduce.5.cloned.1.call-update) | async-done | bytes 262160 | tf_op jit(solution)/shard_map/psum | solution.py:11
  153.2 2048.1 %while.28 = (s32[]{:T(128)}, f32[4,512,128]{2,1,0:T(8,128)S(1)}, f32[512,128]{1,0:T(8,128)S(1)}, s32[]{:T(128)}, s32[]{:T(128)}, /*index=5*/f32[4,2,512,512]{2,3...) while((s32[]{:T(128)}, f32[4,512,128]{2,1,0:T(8,128)S(1)}, ...), condition=%wide.region_12.14_spmd.clone.clone, body=%wide.region_3.13_spmd.clone.clone.sunk | while | flops 2266480640 | bytes 54005560 | solution.py:116
  163.3 40.6 %all-reduce.9.cloned.1.call-done = f32[512,128]{1,0:T(8,128)} async-done(((f32[512,128]{1,0:T(8,128)}), f32[512,128]{1,0:T(8,128)}) %all-reduce.9.cloned.1.call-update) | async-done | bytes 262160 | tf_op jit(solution)/shard_map/while/body/eval_jaxpr/psum | solution.py:112
  204.9 86.8 %all-reduce.7.cloned.1.call-done = f32[512,128]{1,0:T(8,128)} async-done(((f32[512,128]{1,0:T(8,128)}), f32[512,128]{1,0:T(8,128)}) %all-reduce.7.cloned.1.call-update) | async-done | bytes 262160 | tf_op jit(solution)/shard_map/while/body/eval_jaxpr/psum | solution.py:11
  300.8 39.6 %all-reduce.9.cloned.1.call-done = f32[512,128]{1,0:T(8,128)} async-done(((f32[512,128]{1,0:T(8,128)}), f32[512,128]{1,0:T(8,128)}) %all-reduce.9.cloned.1.call-update) | async-done | bytes 262160 | tf_op jit(solution)/shard_map/while/body/eval_jaxpr/psum | solution.py:112
  341.4 85.4 %all-reduce.7.cloned.1.call-done = f32[512,128]{1,0:T(8,128)} async-done(((f32[512,128]{1,0:T(8,128)}), f32[512,128]{1,0:T(8,128)}) %all-reduce.7.cloned.1.call-update) | async-done | bytes 262160 | tf_op jit(solution)/shard_map/while/body/eval_jaxpr/psum | solution.py:11
  435.9 40.6 %all-reduce.9.cloned.1.call-done = f32[512,128]{1,0:T(8,128)} async-done(((f32[512,128]{1,0:T(8,128)}), f32[512,128]{1,0:T(8,128)}) %all-reduce.9.cloned.1.call-update) | async-done | bytes 262160 | tf_op jit(solution)/shard_map/while/body/eval_jaxpr/psum | solution.py:112
  477.4 85.9 %all-reduce.7.cloned.1.call-done = f32[512,128]{1,0:T(8,128)} async-done(((f32[512,128]{1,0:T(8,128)}), f32[512,128]{1,0:T(8,128)}) %all-reduce.7.cloned.1.call-update) | async-done | bytes 262160 | tf_op jit(solution)/shard_map/while/body/eval_jaxpr/psum | solution.py:11
  572.6 37.7 %all-reduce.9.cloned.1.call-done = f32[512,128]{1,0:T(8,128)} async-done(((f32[512,128]{1,0:T(8,128)}), f32[512,128]{1,0:T(8,128)}) %all-reduce.9.cloned.1.call-update) | async-done | bytes 262160 | tf_op jit(solution)/shard_map/while/body/eval_jaxpr/psum | solution.py:112
  611.3 88.0 %all-reduce.7.cloned.1.call-done = f32[512,128]{1,0:T(8,128)} async-done(((f32[512,128]{1,0:T(8,128)}), f32[512,128]{1,0:T(8,128)}) %all-reduce.7.cloned.1.call-update) | async-done | bytes 262160 | tf_op jit(solution)/shard_map/while/body/eval_jaxpr/psum | solution.py:11
  709.4 40.6 %all-reduce.9.cloned.1.call-done = f32[512,128]{1,0:T(8,128)} async-done(((f32[512,128]{1,0:T(8,128)}), f32[512,128]{1,0:T(8,128)}) %all-reduce.9.cloned.1.call-update) | async-done | bytes 262160 | tf_op jit(solution)/shard_map/while/body/eval_jaxpr/psum | solution.py:112
  751.0 86.8 %all-reduce.7.cloned.1.call-done = f32[512,128]{1,0:T(8,128)} async-done(((f32[512,128]{1,0:T(8,128)}), f32[512,128]{1,0:T(8,128)}) %all-reduce.7.cloned.1.call-update) | async-done | bytes 262160 | tf_op jit(solution)/shard_map/while/body/eval_jaxpr/psum | solution.py:11
  841.4 5.7 conditional.16
  841.4 5.7 fusion.11
  848.8 37.8 %all-reduce.9.cloned.1.call-done = f32[512,128]{1,0:T(8,128)} async-done(((f32[512,128]{1,0:T(8,128)}), f32[512,128]{1,0:T(8,128)}) %all-reduce.9.cloned.1.call-update) | async-done | bytes 262160 | tf_op jit(solution)/shard_map/while/body/eval_jaxpr/psum | solution.py:112
  887.5 85.3 %all-reduce.7.cloned.1.call-done = f32[512,128]{1,0:T(8,128)} async-done(((f32[512,128]{1,0:T(8,128)}), f32[512,128]{1,0:T(8,128)}) %all-reduce.7.cloned.1.call-update) | async-done | bytes 262160 | tf_op jit(solution)/shard_map/while/body/eval_jaxpr/psum | solution.py:11
  977.3 15.6 collective-permute-done
  992.9 65.2 %conditional.15 = (f32[512,128]{1,0:T(8,128)S(1)}) conditional(s32[]{:T(128)} %convert_element_type.68, () %tuple.144, (s32[]{:T(128)}, s32[]{:T(128)}, f32[4,2,512,512]{2,3,0,1:T(8,128)}, s32[]{:T(128)}, pred[]{:T(512)}, /*index=5*/pred[]{:T(512)}, s32[]{:T(128)}, f32[2,512,128]{2,1,0:T(8,128)}, f32[512,128]{1,0:T(8,128)S(1)}, ...), branch_computations={%region_6.7_spmd, %region_7.8_spmd} | conditional | flops 252690464 | bytes 22546512 | solution.py:76
  992.9 10.0 copy.8
  1004.2 10.6 while.27
  1014.8 40.1 %custom-call.5 = f32[4,128,128]{1,2,0:T(8,128)S(1)} custom-call(f32[4,128,128]{2,1,0:T(8,128)} %get-tuple-element.560), custom_call_target="InvertDiagBlocksLowerTriangular" | custom-call | tf_op jit(solution)/shard_map/while/body/eval_jaxpr/cond/branch_1_fun/triangular_solve/custom-call.1 | solution.py:72
  1059.8 48.9 %all-reduce.7.cloned.1.call-done = f32[512,128]{1,0:T(8,128)} async-done(((f32[512,128]{1,0:T(8,128)}), f32[512,128]{1,0:T(8,128)}) %all-reduce.7.cloned.1.call-update) | async-done | bytes 262160 | tf_op jit(solution)/shard_map/while/body/eval_jaxpr/psum | solution.py:11
  1118.0 37.9 %all-reduce.9.cloned.1.call-done = f32[512,128]{1,0:T(8,128)} async-done(((f32[512,128]{1,0:T(8,128)}), f32[512,128]{1,0:T(8,128)}) %all-reduce.9.cloned.1.call-update) | async-done | bytes 262160 | tf_op jit(solution)/shard_map/while/body/eval_jaxpr/psum | solution.py:112
  1156.9 88.0 %all-reduce.7.cloned.1.call-done = f32[512,128]{1,0:T(8,128)} async-done(((f32[512,128]{1,0:T(8,128)}), f32[512,128]{1,0:T(8,128)}) %all-reduce.7.cloned.1.call-update) | async-done | bytes 262160 | tf_op jit(solution)/shard_map/while/body/eval_jaxpr/psum | solution.py:11
  1255.0 40.6 %all-reduce.9.cloned.1.call-done = f32[512,128]{1,0:T(8,128)} async-done(((f32[512,128]{1,0:T(8,128)}), f32[512,128]{1,0:T(8,128)}) %all-reduce.9.cloned.1.call-update) | async-done | bytes 262160 | tf_op jit(solution)/shard_map/while/body/eval_jaxpr/psum | solution.py:112
  1296.5 86.8 %all-reduce.7.cloned.1.call-done = f32[512,128]{1,0:T(8,128)} async-done(((f32[512,128]{1,0:T(8,128)}), f32[512,128]{1,0:T(8,128)}) %all-reduce.7.cloned.1.call-update) | async-done | bytes 262160 | tf_op jit(solution)/shard_map/while/body/eval_jaxpr/psum | solution.py:11
  1392.5 39.6 %all-reduce.9.cloned.1.call-done = f32[512,128]{1,0:T(8,128)} async-done(((f32[512,128]{1,0:T(8,128)}), f32[512,128]{1,0:T(8,128)}) %all-reduce.9.cloned.1.call-update) | async-done | bytes 262160 | tf_op jit(solution)/shard_map/while/body/eval_jaxpr/psum | solution.py:112
  1433.0 85.3 %all-reduce.7.cloned.1.call-done = f32[512,128]{1,0:T(8,128)} async-done(((f32[512,128]{1,0:T(8,128)}), f32[512,128]{1,0:T(8,128)}) %all-reduce.7.cloned.1.call-update) | async-done | bytes 262160 | tf_op jit(solution)/shard_map/while/body/eval_jaxpr/psum | solution.py:11
  1527.5 40.6 %all-reduce.9.cloned.1.call-done = f32[512,128]{1,0:T(8,128)} async-done(((f32[512,128]{1,0:T(8,128)}), f32[512,128]{1,0:T(8,128)}) %all-reduce.9.cloned.1.call-update) | async-done | bytes 262160 | tf_op jit(solution)/shard_map/while/body/eval_jaxpr/psum | solution.py:112
  1569.1 85.9 %all-reduce.7.cloned.1.call-done = f32[512,128]{1,0:T(8,128)} async-done(((f32[512,128]{1,0:T(8,128)}), f32[512,128]{1,0:T(8,128)}) %all-reduce.7.cloned.1.call-update) | async-done | bytes 262160 | tf_op jit(solution)/shard_map/while/body/eval_jaxpr/psum | solution.py:11
  1664.2 37.7 %all-reduce.9.cloned.1.call-done = f32[512,128]{1,0:T(8,128)} async-done(((f32[512,128]{1,0:T(8,128)}), f32[512,128]{1,0:T(8,128)}) %all-reduce.9.cloned.1.call-update) | async-done | bytes 262160 | tf_op jit(solution)/shard_map/while/body/eval_jaxpr/psum | solution.py:112
  1702.9 88.1 %all-reduce.7.cloned.1.call-done = f32[512,128]{1,0:T(8,128)} async-done(((f32[512,128]{1,0:T(8,128)}), f32[512,128]{1,0:T(8,128)}) %all-reduce.7.cloned.1.call-update) | async-done | bytes 262160 | tf_op jit(solution)/shard_map/while/body/eval_jaxpr/psum | solution.py:11
  1801.1 40.6 %all-reduce.9.cloned.1.call-done = f32[512,128]{1,0:T(8,128)} async-done(((f32[512,128]{1,0:T(8,128)}), f32[512,128]{1,0:T(8,128)}) %all-reduce.9.cloned.1.call-update) | async-done | bytes 262160 | tf_op jit(solution)/shard_map/while/body/eval_jaxpr/psum | solution.py:112
  1842.6 86.8 %all-reduce.7.cloned.1.call-done = f32[512,128]{1,0:T(8,128)} async-done(((f32[512,128]{1,0:T(8,128)}), f32[512,128]{1,0:T(8,128)}) %all-reduce.7.cloned.1.call-update) | async-done | bytes 262160 | tf_op jit(solution)/shard_map/while/body/eval_jaxpr/psum | solution.py:11
  1933.0 5.7 conditional.16
  1940.4 37.8 %all-reduce.9.cloned.1.call-done = f32[512,128]{1,0:T(8,128)} async-done(((f32[512,128]{1,0:T(8,128)}), f32[512,128]{1,0:T(8,128)}) %all-reduce.9.cloned.1.call-update) | async-done | bytes 262160 | tf_op jit(solution)/shard_map/while/body/eval_jaxpr/psum | solution.py:112
  1979.1 85.3 %all-reduce.7.cloned.1.call-done = f32[512,128]{1,0:T(8,128)} async-done(((f32[512,128]{1,0:T(8,128)}), f32[512,128]{1,0:T(8,128)}) %all-reduce.7.cloned.1.call-update) | async-done | bytes 262160 | tf_op jit(solution)/shard_map/while/body/eval_jaxpr/psum | solution.py:11
  2068.1 5.7 conditional.16
  2074.6 9.9 collective-permute-done
  2084.6 65.1 %conditional.15 = (f32[512,128]{1,0:T(8,128)S(1)}) conditional(s32[]{:T(128)} %convert_element_type.68, () %tuple.144, (s32[]{:T(128)}, s32[]{:T(128)}, f32[4,2,512,512]{2,3,0,1:T(8,128)}, s32[]{:T(128)}, pred[]{:T(512)}, /*index=5*/pred[]{:T(512)}, s32[]{:T(128)}, f32[2,512,128]{2,1,0:T(8,128)}, f32[512,128]{1,0:T(8,128)S(1)}, ...), branch_computations={%region_6.7_spmd, %region_7.8_spmd} | conditional | flops 252690464 | bytes 22546512 | solution.py:76
  2084.6 10.0 copy.8
  2095.9 10.6 while.27
  2106.5 40.1 %custom-call.5 = f32[4,128,128]{1,2,0:T(8,128)S(1)} custom-call(f32[4,128,128]{2,1,0:T(8,128)} %get-tuple-element.560), custom_call_target="InvertDiagBlocksLowerTriangular" | custom-call | tf_op jit(solution)/shard_map/while/body/eval_jaxpr/cond/branch_1_fun/triangular_solve/custom-call.1 | solution.py:72
  2151.5 48.9 %all-reduce.7.cloned.1.call-done = f32[512,128]{1,0:T(8,128)} async-done(((f32[512,128]{1,0:T(8,128)}), f32[512,128]{1,0:T(8,128)}) %all-reduce.7.cloned.1.call-update) | async-done | bytes 262160 | tf_op jit(solution)/shard_map/while/body/eval_jaxpr/psum | solution.py:11
  2201.4 11.0 fusion.55
  (350 shorter events, 182.1 us)
Async XLA Ops:
  7.2 2194.2 %copy-start = (f32[2,1,512,128]{3,2,1,0:T(8,128)S(1)}, f32[2,1,512,128]{3,2,1,0:T(8,128)}, u32[]{:S(2)}) copy-start(f32[2,1,512,128]{3,2,1,0:T(8,128)} %param.20) | copy-start | bytes 1572868
  7.2 145.9 %all-reduce.5.cloned.1.call-start = ((), (), s32[]{:S(2)}) async-start(), calls=%async_computation | async-start | bytes 524288 | tf_op jit(solution)/shard_map/psum | solution.py:11
  7.2 17.2 copy-start.3
  153.3 50.7 %all-reduce.9.cloned.1.call-start = ((), (), s32[]{:S(2)}) async-start(), calls=%async_computation.2 | async-start | bytes 524288 | tf_op jit(solution)/shard_map/while/body/eval_jaxpr/psum | solution.py:112
  153.4 9.1 collective-permute-start
  158.5 133.2 %all-reduce.7.cloned.1.call-start = ((), (), s32[]{:S(2)}) async-start(), calls=%async_computation.1 | async-start | bytes 524288 | tf_op jit(solution)/shard_map/while/body/eval_jaxpr/psum | solution.py:11
  291.7 48.7 %all-reduce.9.cloned.1.call-start = ((), (), s32[]{:S(2)}) async-start(), calls=%async_computation.2 | async-start | bytes 524288 | tf_op jit(solution)/shard_map/while/body/eval_jaxpr/psum | solution.py:112
  291.9 8.1 collective-permute-start
  296.0 130.7 %all-reduce.7.cloned.1.call-start = ((), (), s32[]{:S(2)}) async-start(), calls=%async_computation.1 | async-start | bytes 524288 | tf_op jit(solution)/shard_map/while/body/eval_jaxpr/psum | solution.py:11
  426.8 49.7 %all-reduce.9.cloned.1.call-start = ((), (), s32[]{:S(2)}) async-start(), calls=%async_computation.2 | async-start | bytes 524288 | tf_op jit(solution)/shard_map/while/body/eval_jaxpr/psum | solution.py:112
  426.9 8.1 collective-permute-start
  431.1 132.2 %all-reduce.7.cloned.1.call-start = ((), (), s32[]{:S(2)}) async-start(), calls=%async_computation.1 | async-start | bytes 524288 | tf_op jit(solution)/shard_map/while/body/eval_jaxpr/psum | solution.py:11
  564.3 46.0 %all-reduce.9.cloned.1.call-start = ((), (), s32[]{:S(2)}) async-start(), calls=%async_computation.2 | async-start | bytes 524288 | tf_op jit(solution)/shard_map/while/body/eval_jaxpr/psum | solution.py:112
  564.5 7.3 collective-permute-start
  567.7 131.6 %all-reduce.7.cloned.1.call-start = ((), (), s32[]{:S(2)}) async-start(), calls=%async_computation.1 | async-start | bytes 524288 | tf_op jit(solution)/shard_map/while/body/eval_jaxpr/psum | solution.py:11
  699.4 50.6 %all-reduce.9.cloned.1.call-start = ((), (), s32[]{:S(2)}) async-start(), calls=%async_computation.2 | async-start | bytes 524288 | tf_op jit(solution)/shard_map/while/body/eval_jaxpr/psum | solution.py:112
  699.5 9.1 collective-permute-start
  704.6 133.1 %all-reduce.7.cloned.1.call-start = ((), (), s32[]{:S(2)}) async-start(), calls=%async_computation.1 | async-start | bytes 524288 | tf_op jit(solution)/shard_map/while/body/eval_jaxpr/psum | solution.py:11
  837.8 48.7 %all-reduce.9.cloned.1.call-start = ((), (), s32[]{:S(2)}) async-start(), calls=%async_computation.2 | async-start | bytes 524288 | tf_op jit(solution)/shard_map/while/body/eval_jaxpr/psum | solution.py:112
  838.0 10.0 collective-permute-start
  847.8 125.0 %all-reduce.7.cloned.1.call-start = ((), (), s32[]{:S(2)}) async-start(), calls=%async_computation.1 | async-start | bytes 524288 | tf_op jit(solution)/shard_map/while/body/eval_jaxpr/psum | solution.py:11
  972.9 86.0 %all-reduce.9.cloned.1.call-start = ((), (), s32[]{:S(2)}) async-start(), calls=%async_computation.2 | async-start | bytes 524288 | tf_op jit(solution)/shard_map/while/body/eval_jaxpr/psum | solution.py:112
  973.0 19.9 collective-permute-start
  977.2 131.5 %all-reduce.7.cloned.1.call-start = ((), (), s32[]{:S(2)}) async-start(), calls=%async_computation.1 | async-start | bytes 524288 | tf_op jit(solution)/shard_map/while/body/eval_jaxpr/psum | solution.py:11
  1109.7 46.2 %all-reduce.9.cloned.1.call-start = ((), (), s32[]{:S(2)}) async-start(), calls=%async_computation.2 | async-start | bytes 524288 | tf_op jit(solution)/shard_map/while/body/eval_jaxpr/psum | solution.py:112
  1109.9 7.3 collective-permute-start
  1113.1 131.8 %all-reduce.7.cloned.1.call-start = ((), (), s32[]{:S(2)}) async-start(), calls=%async_computation.1 | async-start | bytes 524288 | tf_op jit(solution)/shard_map/while/body/eval_jaxpr/psum | solution.py:11
  1244.9 50.7 %all-reduce.9.cloned.1.call-start = ((), (), s32[]{:S(2)}) async-start(), calls=%async_computation.2 | async-start | bytes 524288 | tf_op jit(solution)/shard_map/while/body/eval_jaxpr/psum | solution.py:112
  1245.1 9.1 collective-permute-start
  1250.2 133.2 %all-reduce.7.cloned.1.call-start = ((), (), s32[]{:S(2)}) async-start(), calls=%async_computation.1 | async-start | bytes 524288 | tf_op jit(solution)/shard_map/while/body/eval_jaxpr/psum | solution.py:11
  1383.4 48.7 %all-reduce.9.cloned.1.call-start = ((), (), s32[]{:S(2)}) async-start(), calls=%async_computation.2 | async-start | bytes 524288 | tf_op jit(solution)/shard_map/while/body/eval_jaxpr/psum | solution.py:112
  1383.5 8.1 collective-permute-start
  1387.7 130.7 %all-reduce.7.cloned.1.call-start = ((), (), s32[]{:S(2)}) async-start(), calls=%async_computation.1 | async-start | bytes 524288 | tf_op jit(solution)/shard_map/while/body/eval_jaxpr/psum | solution.py:11
  1518.4 49.7 %all-reduce.9.cloned.1.call-start = ((), (), s32[]{:S(2)}) async-start(), calls=%async_computation.2 | async-start | bytes 524288 | tf_op jit(solution)/shard_map/while/body/eval_jaxpr/psum | solution.py:112
  1518.6 8.1 collective-permute-start
  1522.7 132.2 %all-reduce.7.cloned.1.call-start = ((), (), s32[]{:S(2)}) async-start(), calls=%async_computation.1 | async-start | bytes 524288 | tf_op jit(solution)/shard_map/while/body/eval_jaxpr/psum | solution.py:11
  1656.0 46.0 %all-reduce.9.cloned.1.call-start = ((), (), s32[]{:S(2)}) async-start(), calls=%async_computation.2 | async-start | bytes 524288 | tf_op jit(solution)/shard_map/while/body/eval_jaxpr/psum | solution.py:112
  1656.1 7.3 collective-permute-start
  1659.3 131.6 %all-reduce.7.cloned.1.call-start = ((), (), s32[]{:S(2)}) async-start(), calls=%async_computation.1 | async-start | bytes 524288 | tf_op jit(solution)/shard_map/while/body/eval_jaxpr/psum | solution.py:11
  1791.0 50.6 %all-reduce.9.cloned.1.call-start = ((), (), s32[]{:S(2)}) async-start(), calls=%async_computation.2 | async-start | bytes 524288 | tf_op jit(solution)/shard_map/while/body/eval_jaxpr/psum | solution.py:112
  1791.2 9.1 collective-permute-start
  1796.3 133.1 %all-reduce.7.cloned.1.call-start = ((), (), s32[]{:S(2)}) async-start(), calls=%async_computation.1 | async-start | bytes 524288 | tf_op jit(solution)/shard_map/while/body/eval_jaxpr/psum | solution.py:11
  1929.5 48.7 %all-reduce.9.cloned.1.call-start = ((), (), s32[]{:S(2)}) async-start(), calls=%async_computation.2 | async-start | bytes 524288 | tf_op jit(solution)/shard_map/while/body/eval_jaxpr/psum | solution.py:112
  1929.6 9.9 collective-permute-start
  1939.4 125.0 %all-reduce.7.cloned.1.call-start = ((), (), s32[]{:S(2)}) async-start(), calls=%async_computation.1 | async-start | bytes 524288 | tf_op jit(solution)/shard_map/while/body/eval_jaxpr/psum | solution.py:11
  2064.5 86.0 %all-reduce.9.cloned.1.call-start = ((), (), s32[]{:S(2)}) async-start(), calls=%async_computation.2 | async-start | bytes 524288 | tf_op jit(solution)/shard_map/while/body/eval_jaxpr/psum | solution.py:112
  2064.7 19.9 collective-permute-start
  2074.5 125.8 %all-reduce.7.cloned.1.call-start = ((), (), s32[]{:S(2)}) async-start(), calls=%async_computation.1 | async-start | bytes 524288 | tf_op jit(solution)/shard_map/while/body/eval_jaxpr/psum | solution.py:11
  (16 other events, 22.0 us)
Sparse Core Ops, SparseCore 0:
  35.2 117.8 all-reduce.4
  158.6 45.2 all-reduce.8
  207.6 84.0 all-reduce.6
  296.2 44.2 all-reduce.8
  343.9 82.7 all-reduce.6
  431.2 45.2 all-reduce.8
  480.1 83.1 all-reduce.6
  567.8 42.4 all-reduce.8
  614.0 85.3 all-reduce.6
  704.8 45.2 all-reduce.8
  753.7 84.0 all-reduce.6
  847.9 38.5 all-reduce.8
  890.2 82.6 all-reduce.6
  977.3 44.9 all-reduce.8
  1058.9 49.7 all-reduce.6
  1113.2 42.6 all-reduce.8
  1159.4 85.4 all-reduce.6
  1250.3 45.2 all-reduce.8
  1299.2 84.0 all-reduce.6
  1387.8 44.2 all-reduce.8
  1435.7 82.6 all-reduce.6
  1522.8 45.2 all-reduce.8
  1571.7 83.1 all-reduce.6
  1659.5 42.4 all-reduce.8
  1705.6 85.3 all-reduce.6
  1796.4 45.2 all-reduce.8
  1845.1 84.2 all-reduce.6
  1939.6 38.5 all-reduce.8
  1981.8 82.6 all-reduce.6
  2074.7 45.0 all-reduce.8
  2150.6 49.7 all-reduce.6
where the time goes:
time: 2220 us
  waiting for transfers between devices  1920 us (86%)
  other arithmetic  111 us (5%)
  local copies, waits for them, and re-layouts  84.6 us (4%)
  starting transfers between devices  53 us (2%)
  matrix products  32.1 us (1%)
    psum x16, waiting for transfers between devices, broadcast(): return lax.psum(jnp.where(mine, value, jnp.zeros_like(value)), axis)  1340 us
    psum x15, waiting for transfers between devices, sweep_step(): next_sum = lax.psum(next_partial, 'row')  512 us
    another operation x10, other arithmetic, solve_here(): lax.linalg.triangular_solve(diagonal, right_side, left_side=True, lower=T...  83 us
    ppermute x15, waiting for transfers between devices, from_behind(): lax.ppermute(value, axis, [(i, (i + by) % size) for i in range(size)])  68.5 us
    ppermute x15, starting transfers between devices, from_behind(): lax.ppermute(value, axis, [(i, (i + by) % size) for i in range(size)])  51.7 us
  transfers between devices with their start and end apart: 46, of which 42 were waited for; matrix products, arithmetic and copies ran while one was open for 8% of the time, Pallas kernels for 0%

commit v1 on v0

v1 whole, which is shorter than its diff:
```python
import functools

import jax
import jax.numpy as jnp
from jax import lax
from jax.experimental import pallas as pl
from jax.experimental.pallas import tpu as pltpu
from jax.sharding import PartitionSpec as P

HIGHEST_PRECISION = lax.Precision.HIGHEST
PRODUCT_PRECISION = lax.Precision.HIGH
BASE_BLOCK = 128
MESH = pl.DeviceIdType.MESH


def lower_mask(row_index, col_index, tile_width):
    inner_mask = lax.broadcasted_iota(
        jnp.int32, (tile_width, tile_width), 0
    ) >= lax.broadcasted_iota(jnp.int32, (tile_width, tile_width), 1)
    return (row_index > col_index) | (row_index == col_index) & inner_mask


def matmul(a, b):
    return jnp.dot(a, b, precision=HIGHEST_PRECISION, preferred_element_type=jnp.float32)


def invert_kernel(tile_ref, inverse_ref):
    width = tile_ref.shape[1]
    base = min(BASE_BLOCK, width)
    row = lax.broadcasted_iota(jnp.int32, (base, base), 0)
    col = lax.broadcasted_iota(jnp.int32, (base, base), 1)
    starts = range(0, width, base)
    blocks = [tile_ref[0, at:at + base, at:at + base] for at in starts]
    inverses = [jnp.where(row == col, 1.0 / jnp.where(row == col, b, 1.0), 0.0) for b in blocks]
    size = 1
    while size < base:
        corner = (row // (2 * size) == col // (2 * size)) & (row // size > col // size)
        halves = [matmul(x, jnp.where(corner, b, 0.0)) for x, b in zip(inverses, blocks)]
        inverses = [x - matmul(h, x) for x, h in zip(inverses, halves)]
        size *= 2
    inverse_ref[0] = jnp.zeros((width, width), jnp.float32)
    for at, x in zip(starts, inverses):
        inverse_ref[0, at:at + base, at:at + base] = x
    while size < width:
        for at in range(0, width, 2 * size):
            top, low = slice(at, at + size), slice(at + size, at + 2 * size)
            half = matmul(inverse_ref[0, low, low], tile_ref[0, low, top])
            inverse_ref[0, low, top] = -matmul(half, inverse_ref[0, top, top])
        size *= 2


def invert(tiles):
    block = pl.BlockSpec((1,) + tiles.shape[1:], lambda s: (s, 0, 0))
    return pl.pallas_call(
        invert_kernel,
        grid=(tiles.shape[0],),
        in_specs=[block],
        out_specs=block,
        out_shape=jax.ShapeDtypeStruct(tiles.shape, jnp.float32),
    )(tiles)


def sweep_kernel(
    rows, cols, tiles_ref, inverse_ref, below_ref, target_ref, solved_ref,
    chain, total, parts, chain_send, plane_send, part_send, chain_recv, plane_recv, part_recv,
):
    my_row, my_col = lax.axis_index("row"), lax.axis_index("col")
    local_rows, local_cols = tiles_ref.shape[0], tiles_ref.shape[1]
    count = local_rows * rows
    gaps = [d for d in range(2, rows + 2) if d != rows]

    def away(row_step, col_step):
        return (lax.rem(my_row + row_step + rows, rows), lax.rem(my_col + col_step + cols, cols))

    partners = [away(0, o) for o in range(1, cols)] + [away(o, 0) for o in range(1, rows)]
    partners += [away(1, 1), away(-1, -1)]
    barrier = pltpu.get_barrier_semaphore()
    for partner in partners:
        pl.semaphore_signal(barrier, inc=1, device_id=partner, device_id_type=MESH)
    pl.semaphore_wait(barrier, len(partners))

    total[...] = jnp.zeros_like(total)

    def chain_copy(slot, landing):
        return pltpu.make_async_remote_copy(
            src_ref=solved_ref.at[slot], dst_ref=chain.at[landing],
            send_sem=chain_send.at[slot], recv_sem=chain_recv.at[landing],
            device_id=away(-1, -1), device_id_type=MESH,
        )

    def plane_copy(slot, offset):
        return pltpu.make_async_remote_copy(
            src_ref=solved_ref.at[slot], dst_ref=solved_ref.at[slot],
            send_sem=plane_send.at[slot, offset], recv_sem=plane_recv.at[slot],
            device_id=away(0, -offset), device_id_type=MESH,
        )

    def part_copy(slot, where, gap):
        return pltpu.make_async_remote_copy(
            src_ref=total.at[slot], dst_ref=parts.at[slot, where],
            send_sem=part_send.at[slot], recv_sem=part_recv.at[slot, where],
            device_id=away((-gap) % rows, 0), device_id_type=MESH,
        )

    plane_order = list(range(2, cols)) + [1]

    def step(offset, carry):
        j = count - 1 - offset
        slot, col_slot = j // rows, j // cols
        on_plane = my_row == lax.rem(j, rows)
        owner = on_plane & (my_col == lax.rem(j, cols))

        @pl.when(owner)
        def _():
            total[col_slot] = target_ref[col_slot] - total[col_slot]
            for where, gap in enumerate(gaps):
                @pl.when(j + gap < count)
                def _():
                    part_copy(col_slot, where, gap).wait_recv()
                    total[col_slot] = total[col_slot] - parts[col_slot, where]
            solved_ref[slot] = matmul(total[col_slot], inverse_ref[col_slot])

            @pl.when(j + 1 < count)
            def _():
                chain_copy(slot, col_slot).wait_recv()
                solved_ref[slot] = solved_ref[slot] - matmul(chain[col_slot], below_ref[col_slot])

            @pl.when(j > 0)
            def _():
                chain_copy(slot, (j - 1) // cols).start()
            for o in plane_order:
                plane_copy(slot, o).start()

        @pl.when(on_plane & jnp.logical_not(owner))
        def _():
            plane_copy(slot, 1).wait_recv()

        @pl.when(on_plane)
        def _():
            for s in reversed(range(local_cols)):
                k = my_col + cols * s

                @pl.when(k < j - 1)
                def _():
                    total[s] = total[s] + matmul(solved_ref[slot], tiles_ref[slot, s])
                for where, gap in enumerate(gaps):
                    @pl.when(k == j - gap)
                    def _():
                        part_copy(s, where, gap).start()
        return carry

    lax.fori_loop(0, count, step, 0)

    def drain(offset, carry):
        j = count - 1 - offset
        slot = j // rows
        on_plane = my_row == lax.rem(j, rows)

        @pl.when(on_plane & (my_col == lax.rem(j, cols)))
        def _():
            @pl.when(j > 0)
            def _():
                chain_copy(slot, 0).wait_send()
            for o in plane_order:
                plane_copy(slot, o).wait_send()

        @pl.when(on_plane)
        def _():
            for s in range(local_cols):
                for where, gap in enumerate(gaps):
                    @pl.when(my_col + cols * s == j - gap)
                    def _():
                        part_copy(s, where, gap).wait_send()
        return carry

    lax.fori_loop(0, count, drain, 0)


def sweep(rows, cols, tiles, inverse, below, target):
    local_rows, local_cols, width = tiles.shape[0], tiles.shape[1], tiles.shape[2]
    rhs = target.shape[1]
    vmem = pl.BlockSpec(memory_space=pltpu.VMEM)
    dma = pltpu.SemaphoreType.DMA
    return pl.pallas_call(
        functools.partial(sweep_kernel, rows, cols),
        out_shape=jax.ShapeDtypeStruct((local_rows, rhs, width), jnp.float32),
        in_specs=[vmem] * 4,
        out_specs=vmem,
        scratch_shapes=[
            pltpu.VMEM((local_cols, rhs, width), jnp.float32),
            pltpu.VMEM((local_cols, rhs, width), jnp.float32),
            pltpu.VMEM((local_cols, rows - 1, rhs, width), jnp.float32),
            dma((local_rows,)),
            dma((local_rows, cols)),
            dma((local_cols,)),
            dma((local_cols,)),
            dma((local_rows,)),
            dma((local_cols, rows - 1)),
        ],
        compiler_params=pltpu.CompilerParams(collective_id=0, has_side_effects=True),
    )(tiles, inverse, below, target)


def body(factor_wide, factor_narrow, flags, forward_solution, solution_grad):
    row_count = lax.axis_size("row")
    col_count = lax.axis_size("col")
    my_row = lax.axis_index("row")
    my_col = lax.axis_index("col")
    local_rows = factor_wide.shape[0]
    local_cols = factor_wide.shape[2]
    tile_width = factor_wide.shape[4]
    tile_count = local_rows * row_count

    def pick(row_slot, col_slot):
        def cut(pool):
            return lax.dynamic_index_in_dim(pool[:, 0, col_slot, 0], row_slot, 0, keepdims=False)
        narrow = cut(flags) == 1
        return jnp.where(narrow, cut(factor_narrow).astype(jnp.float32), cut(factor_wide))

    targets = [my_col + col_count * s for s in range(local_cols)]
    below = jnp.stack([
        pick(jnp.minimum(j + 1, tile_count - 1) // row_count, s) for s, j in enumerate(targets)
    ])
    below = lax.ppermute(below, "row", [(i, (i - 1) % row_count) for i in range(row_count)])
    factor_tiles = jnp.where(
        flags[:, 0, :, 0, None, None] == 1,
        factor_narrow[:, 0, :, 0].astype(jnp.float32),
        factor_wide[:, 0, :, 0],
    )
    diagonal = jnp.stack([pick(j // row_count, s) for s, j in enumerate(targets)])
    inverse = invert(diagonal)
    correction = jnp.einsum(
        "sab,sbc->sac", below, inverse, precision=HIGHEST_PRECISION,
        preferred_element_type=jnp.float32,
    )
    target = jnp.swapaxes(solution_grad[:, 0], 1, 2)
    solved = sweep(row_count, col_count, factor_tiles, inverse, correction, target)
    row_index = jnp.arange(local_rows, dtype=jnp.int32) * row_count + my_row
    col_index = jnp.arange(local_cols, dtype=jnp.int32) * col_count + my_col
    products = -jnp.einsum(
        "ark,blr->abkl", solved, forward_solution[:, 0], precision=PRODUCT_PRECISION
    )
    masks = lower_mask(row_index[:, None, None, None], col_index[None, :, None, None], tile_width)
    factor_grad = jnp.where(masks, products, jnp.zeros_like(products))
    return (jnp.swapaxes(solved, 1, 2)[:, None], factor_grad[:, None, :, None])


def solution(mesh):
    placed = (
        P(None, "row", None, "col", None, None),
        P(None, "row", None, "col", None, None),
        P(None, "row", None, "col"),
        P(None, "col", None, None),
        P(None, "col", None, None),
    )
    return jax.shard_map(
        body,
        mesh=mesh,
        in_specs=placed,
        out_specs=(P(None, "row", None, None), P(None, "row", None, "col", None, None)),
        check_vma=False,
    )
```

time: 2220 us -> 208 us (0.09)
  waiting for transfers between devices: 1920 us -> 20.9 us
  Pallas kernels: 0 us -> 140 us
  other arithmetic: 111 us -> 13.7 us
  local copies, waits for them, and re-layouts: 84.6 us -> 10.9 us
  starting transfers between devices: 53 us -> 5.08 us
    psum x31 -> x0, waiting for transfers between devices: 1850 us -> none  [the longest x16 1340 us: broadcast(): return lax.psum(jnp.where(mine, value, jnp.zeros_like(value)), axis)]
    pallas_call x0 -> x2, Pallas kernels: none -> 140 us  [the longest x1 129 us: sweep(): pl.pallas_call(functools.partial(sweep_kernel, rows, cols), out_shape=jax...]
    another operation x10 -> x2, other arithmetic: 83 us -> 2.97 us  [the longest x1 1.49 us: body(): jnp.stack([pick(j // row_count, s) for s, j in enumerate(targets)])]
    ppermute x15 -> x1, waiting for transfers between devices: 68.5 us -> 20.9 us  [body(): lax.ppermute(below, 'row', [(i, (i - 1) % row_count) for i in range(row_c...]
    ppermute x15 -> x1, starting transfers between devices: 51.7 us -> 5.08 us  [body(): lax.ppermute(below, 'row', [(i, (i - 1) % row_count) for i in range(row_c...]
    another operation x70 -> x0, local copies, waits for them, and re-layouts: 41.8 us -> none  [the longest x26 21.2 us: solve_here(): lax.linalg.triangular_solve(diagonal, right_side, left_side=True, lower=T...]
    while x45 -> x0, local copies, waits for them, and re-layouts: 25 us -> none
  transfers between devices with their start and end apart: 46 -> 1, of which waited for: 42 -> 1; matrix products, arithmetic and copies ran while one was open for 8% -> 6% of each run, Pallas kernels for 0% -> 6%
where the time goes in v1:
time: 208 us
  Pallas kernels  140 us (67%)
  waiting for transfers between devices  20.9 us (10%)
  other arithmetic  13.7 us (7%)
  matrix products  13.5 us (6%)
  local copies, waits for them, and re-layouts  10.9 us (5%)
  starting transfers between devices  5.08 us (2%)
  between operations  3.33 us (2%)
    pallas_call x1, Pallas kernels, sweep(): pl.pallas_call(functools.partial(sweep_kernel, rows, cols), out_shape=jax...  129 us
    ppermute x1, waiting for transfers between devices, body(): lax.ppermute(below, 'row', [(i, (i - 1) % row_count) for i in range(row_c...  20.9 us
    pallas_call x1, Pallas kernels, invert(): pl.pallas_call(invert_kernel, grid=(tiles.shape[0],), in_specs=[block], o...  11.8 us
    select_n x1, other arithmetic, body(): jnp.where(flags[:, 0, :, 0, None, None] == 1, factor_narrow[:, 0, :, 0].a...  9.76 us
    dot_general x1, matrix products, body(): jnp.einsum('ark,blr->abkl', solved, forward_solution[:, 0], precision=PRO...  8.69 us
    slice x3, local copies, waits for them, and re-layouts, cut(): pool[:, 0, col_slot, 0]  5.86 us
    ppermute x1, starting transfers between devices, body(): lax.ppermute(below, 'row', [(i, (i - 1) % row_count) for i in range(row_c...  5.08 us
    dot_general x1, matrix products, body(): jnp.einsum('sab,sbc->sac', below, inverse, precision=HIGHEST_PRECISION, p...  4.82 us
  transfers between devices with their start and end apart: 1, of which 1 were waited for; matrix products, arithmetic and copies ran while one was open for 6% of the time, Pallas kernels for 6%

profile of v1, /device:TPU:0, one launch (start us, length us, event | category | flops | bytes accessed | tf_op | source)
XLA Modules:
  0.0 207.8 jit_solution(10183236715720260281)
XLA Ops:
  0.6 0.0 copy-start
  0.7 0.7 fusion.5
  1.4 0.6 constant_dynamic-slice_fusion.1
  3.3 0.7 constant_dynamic-slice_fusion
  5.2 0.0 copy-start.2
  5.2 4.7 %fusion.3 = (f32[4,1,1,1,512,512]{5,4,3,2,1,0:T(8,128)S(1)}, f32[4,1,1,1,512,512]{5,4,3,2,1,0:T(8,128)S(1)}) fusion(f32[4,1,2,1,512,512]{5,4,3,2,1,0:T(8,128)} %param.5), kind=kLoop, calls=%fused_computation.21 | loop fusion | bytes 16777216 | tf_op jit(solution)/shard_map/slice | solution.py:216
  9.9 0.0 copy-done.2
  9.9 0.5 fusion.4
  10.4 0.8 select_bitcast_fusion
  11.2 1.5 pad_maximum_fusion.1
  12.7 5.1 %collective-permute-start = (f32[2,512,512]{2,1,0:T(8,128)}, f32[2,512,512]{2,1,0:T(8,128)S(1)}, u32[]{:S(2)}, u32[]{:S(2)}) collective-permute-start(f32[2,512,512]{2,1,0:T(8,128)} %pad_maximum_fusion.1), channel_id=1, source_target_pairs={{0,24},{8,0},{16,8},{24,16},{1,25},{9,1},{17,9},{25,17},{2,26},{10... | collective-permute-start | bytes 6291464 | tf_op jit(solution)/shard_map/ppermute | solution.py:224
  17.8 1.5 pad_maximum_fusion.tile_ref
  19.3 0.0 copy-start.5
  19.3 0.0 copy-start.4
  19.3 11.8 %shard_map.68.inverse_ref = f32[2,512,512]{2,1,0:T(8,128)} custom-call(f32[2,512,512]{2,1,0:T(8,128)} %pad_maximum_fusion.tile_ref), custom_call_target="tpu_custom_call" | custom-call | tf_op jit(solution)/shard_map/pallas_call | solution.py:54
  31.1 0.0 copy-done.5
  31.1 0.1 copy.7
  31.2 0.0 copy-done.4
  31.2 1.0 copy.9
  32.2 0.1 iota_compare_fusion
  32.3 0.1 broadcast_compare_fusion.1
  32.4 0.0 copy-start.1
  32.4 9.8 %convert_select_fusion.tiles_ref = f32[4,2,512,512]{3,2,1,0:T(8,128)} fusion(f32[4,1,2,1,512,512]{5,4,3,2,1,0:T(8,128)} %param.5, bf16[4,1,2,1,512,512]{5,4,3,2,1,0:T(8,128)(2,1)} %param.6, pred[4,2]{1,0:T(4,128)(4,1)S(1)} %bitcast.47), kind=kLoop, calls=%fused_computation | loop fusion | flops 4194304 | bytes 20971528 | tf_op jit(solution)/shard_map/jit(_where)/select_n | solution.py:225
  42.1 20.9 %collective-permute-done = f32[2,512,512]{2,1,0:T(8,128)S(1)} collective-permute-done((f32[2,512,512]{2,1,0:T(8,128)}, f32[2,512,512]{2,1,0:T(8,128)S(1)}, u32[]{:S(2)}, u32[]{:S(2)}) %collective-permute-start) | collective-permute-done | bytes 2097184 | tf_op jit(solution)/shard_map/ppermute | solution.py:224
  63.0 0.0 copy-done.1
  63.0 4.8 %fusion.6.below_ref = f32[2,512,512]{2,1,0:T(8,128)} fusion(f32[2,512,512]{2,1,0:T(8,128)S(1)} %collective-permute-done, f32[2,512,512]{2,1,0:T(8,128)S(1)} %copy-done.1), kind=kOutput, calls=%fused_computation.24 | convolution fusion | flops 3221225472 | bytes 6291456 | tf_op jit(solution)/shard_map/sab,sbc->sac/dot_general | solution.py:232
  67.8 128.7 %shard_map.69 = f32[4,128,512]{2,1,0:T(8,128)} custom-call(f32[4,2,512,512]{3,2,1,0:T(8,128)} %convert_select_fusion.tiles_ref, f32[2,512,512]{2,1,0:T(8,128)} %shard_map.68.inverse_ref, f32[2,512,512]{2,1,0:T(8,128)} %fusion.6.below_ref, f32[2,128,512]{2,1,0:T(8,128)} %bitcast.46), custom_call_target="tpu_custom_call" | custom-call | tf_op jit(solution)/shard_map/pallas_call | solution.py:184
  196.5 0.0 copy-start.3
  196.5 2.6 %copy.11 = f32[4,1,512,128]{3,2,1,0:T(8,128)} copy(f32[4,1,512,128]{2,3,0,1:T(8,128)} %bitcast.45) | data formatting | bytes 2097152
  199.1 0.0 copy-done
  199.1 0.0 copy-done.3
  199.1 8.7 %fusion = f32[4,1,2,1,512,512]{5,4,3,2,1,0:T(8,128)} fusion(pred[512,512]{1,0:T(8,128)(4,1)S(1)} %iota_compare_fusion, pred[4,2]{1,0:T(4,128)(4,1)S(1)} %get-tuple-element.13, pred[4,2]{1,0:T(4,128)(4,1)S(1)} %get-tuple-element.12, f32[4,128,512]{2,1,0:T(8,128)S(1)} %copy-done.3, f32[2,1,512,128]{3,2,1,0:T(8,128)S(1)} %copy-done), kind=kOutput, calls=%fused_computation.2 | convolution fusion | flops 1619001344 | bytes 10223632 | tf_op jit(solution)/shard_map/ark,blr->abkl/dot_general | solution.py:240
  (3 shorter events, 0.0 us)
Async XLA Ops:
  0.6 198.5 %copy-start = (f32[2,1,512,128]{3,2,1,0:T(8,128)S(1)}, f32[2,1,512,128]{3,2,1,0:T(8,128)}, u32[]{:S(2)}) copy-start(f32[2,1,512,128]{3,2,1,0:T(8,128)} %param.8) | copy-start | bytes 1572868
  5.2 4.7 %copy-start.2 = (bf16[4,1,2,1,512,512]{5,4,3,2,1,0:T(8,128)(2,1)S(1)}, bf16[4,1,2,1,512,512]{5,4,3,2,1,0:T(8,128)(2,1)}, u32[]{:S(2)}) copy-start(bf16[4,1,2,1,512,512]{5,4,3,2,1,0:T(8,128)(2,1)} %param.6) | copy-start | bytes 12582916
  12.7 50.3 %collective-permute-start = (f32[2,512,512]{2,1,0:T(8,128)}, f32[2,512,512]{2,1,0:T(8,128)S(1)}, u32[]{:S(2)}, u32[]{:S(2)}) collective-permute-start(f32[2,512,512]{2,1,0:T(8,128)} %pad_maximum_fusion.1), channel_id=1, source_target_pairs={{0,24},{8,0},{16,8},{24,16},{1,25},{9,1},{17,9},{25,17},{2,26},{10... | collective-permute-start | bytes 6291464 | tf_op jit(solution)/shard_map/ppermute | solution.py:224
  19.3 11.8 %copy-start.5 = (s32[4,1,2,1]{0,3,2,1:T(1,128)S(1)}, s32[4,1,2,1]{0,3,2,1:T(1,128)}, u32[]{:S(2)}) copy-start(s32[4,1,2,1]{0,3,2,1:T(1,128)} %param.7) | copy-start | bytes 100
  19.3 11.9 %copy-start.4 = (f32[2,1,512,128]{3,2,1,0:T(8,128)S(1)}, f32[2,1,512,128]{3,2,1,0:T(8,128)}, u32[]{:S(2)}) copy-start(f32[2,1,512,128]{3,2,1,0:T(8,128)} %param.9) | copy-start | bytes 1572868
  32.4 30.6 %copy-start.1 = (f32[2,512,512]{2,1,0:T(8,128)S(1)}, f32[2,512,512]{2,1,0:T(8,128)}, u32[]{:S(2)}) copy-start(f32[2,512,512]{2,1,0:T(8,128)} %shard_map.68.inverse_ref) | copy-start | bytes 6291460
  196.5 2.6 %copy-start.3 = (f32[4,128,512]{2,1,0:T(8,128)S(1)}, f32[4,128,512]{2,1,0:T(8,128)}, u32[]{:S(2)}) copy-start(f32[4,128,512]{2,1,0:T(8,128)} %shard_map.69) | copy-start | bytes 3145732

commit v2 on v1

--- a/solution.py
+++ b/solution.py
@@ -24,13 +24,27 @@
     return jnp.dot(a, b, precision=HIGHEST_PRECISION, preferred_element_type=jnp.float32)
 
 
+def split(value):
+    high = value.astype(jnp.bfloat16)
+    return high, (value - high.astype(jnp.float32)).astype(jnp.bfloat16)
+
+
+def split_product(value, high, low):
+    count = value.shape[0]
+    value_high, value_low = split(value)
+    both = jnp.concatenate([value_high, value_low], axis=0)
+    first = jnp.dot(both, high, preferred_element_type=jnp.float32)
+    second = jnp.dot(value_high, low, preferred_element_type=jnp.float32)
+    return first[:count] + (first[count:] + second)
+
+
 def invert_kernel(tile_ref, inverse_ref):
-    width = tile_ref.shape[1]
+    width = tile_ref.shape[0]
     base = min(BASE_BLOCK, width)
     row = lax.broadcasted_iota(jnp.int32, (base, base), 0)
     col = lax.broadcasted_iota(jnp.int32, (base, base), 1)
     starts = range(0, width, base)
-    blocks = [tile_ref[0, at:at + base, at:at + base] for at in starts]
+    blocks = [tile_ref[at:at + base, at:at + base] for at in starts]
     inverses = [jnp.where(row == col, 1.0 / jnp.where(row == col, b, 1.0), 0.0) for b in blocks]
     size = 1
     while size < base:
@@ -38,34 +52,32 @@
         halves = [matmul(x, jnp.where(corner, b, 0.0)) for x, b in zip(inverses, blocks)]
         inverses = [x - matmul(h, x) for x, h in zip(inverses, halves)]
         size *= 2
-    inverse_ref[0] = jnp.zeros((width, width), jnp.float32)
+    inverse_ref[...] = jnp.zeros((width, width), jnp.float32)
     for at, x in zip(starts, inverses):
-        inverse_ref[0, at:at + base, at:at + base] = x
+        inverse_ref[at:at + base, at:at + base] = x
     while size < width:
         for at in range(0, width, 2 * size):
             top, low = slice(at, at + size), slice(at + size, at + 2 * size)
-            half = matmul(inverse_ref[0, low, low], tile_ref[0, low, top])
-            inverse_ref[0, low, top] = -matmul(half, inverse_ref[0, top, top])
+            half = matmul(inverse_ref[low, low], tile_ref[low, top])
+            inverse_ref[low, top] = -matmul(half, inverse_ref[top, top])
         size *= 2
 
 
-def invert(tiles):
-    block = pl.BlockSpec((1,) + tiles.shape[1:], lambda s: (s, 0, 0))
+def invert(tile):
     return pl.pallas_call(
-        invert_kernel,
-        grid=(tiles.shape[0],),
-        in_specs=[block],
-        out_specs=block,
-        out_shape=jax.ShapeDtypeStruct(tiles.shape, jnp.float32),
-    )(tiles)
-
-
-def sweep_kernel(
-    rows, cols, tiles_ref, inverse_ref, below_ref, target_ref, solved_ref,
-    chain, total, parts, chain_send, plane_send, part_send, chain_recv, plane_recv, part_recv,
-):
+        invert_kernel, out_shape=jax.ShapeDtypeStruct(tile.shape, jnp.float32)
+    )(tile)
+
+
+def sweep_kernel(rows, cols, tiles_ref, target_ref, *refs):
+    local_cols = tiles_ref.shape[1]
+    inverse_refs, below_refs = refs[:local_cols], refs[local_cols:2 * local_cols]
+    (
+        solved_ref, chain, total, parts, weights, chain_send, plane_send, part_send,
+        chain_recv, plane_recv, part_recv,
+    ) = refs[2 * local_cols:]
     my_row, my_col = lax.axis_index("row"), lax.axis_index("col")
-    local_rows, local_cols = tiles_ref.shape[0], tiles_ref.shape[1]
+    local_rows = tiles_ref.shape[0]
     count = local_rows * rows
     gaps = [d for d in range(2, rows + 2) if d != rows]
 
@@ -80,6 +92,9 @@
     pl.semaphore_wait(barrier, len(partners))
 
     total[...] = jnp.zeros_like(total)
+    for s in range(local_cols):
+        weights[s, 0], weights[s, 1] = split(inverse_refs[s][...])
+        weights[s, 2], weights[s, 3] = split(below_refs[s][...])
 
     def chain_copy(slot, landing):
         return pltpu.make_async_remote_copy(
@@ -118,12 +133,16 @@
                 def _():
                     part_copy(col_slot, where, gap).wait_recv()
                     total[col_slot] = total[col_slot] - parts[col_slot, where]
-            solved_ref[slot] = matmul(total[col_slot], inverse_ref[col_slot])
+            solved_ref[slot] = split_product(
+                total[col_slot], weights[col_slot, 0], weights[col_slot, 1]
+            )
 
             @pl.when(j + 1 < count)
             def _():
                 chain_copy(slot, col_slot).wait_recv()
-                solved_ref[slot] = solved_ref[slot] - matmul(chain[col_slot], below_ref[col_slot])
+                solved_ref[slot] = solved_ref[slot] - split_product(
+                    chain[col_slot], weights[col_slot, 2], weights[col_slot, 3]
+                )
 
             @pl.when(j > 0)
             def _():
@@ -142,7 +161,9 @@
 
                 @pl.when(k < j - 1)
                 def _():
-                    total[s] = total[s] + matmul(solved_ref[slot], tiles_ref[slot, s])
+                    total[s] = total[s] + split_product(
+                        solved_ref[slot], *split(tiles_ref[slot, s])
+                    )
                 for where, gap in enumerate(gaps):
                     @pl.when(k == j - gap)
                     def _():
@@ -176,7 +197,7 @@
     lax.fori_loop(0, count, drain, 0)
 
 
-def sweep(rows, cols, tiles, inverse, below, target):
+def sweep(rows, cols, tiles, target, inverses, corrections):
     local_rows, local_cols, width = tiles.shape[0], tiles.shape[1], tiles.shape[2]
     rhs = target.shape[1]
     vmem = pl.BlockSpec(memory_space=pltpu.VMEM)
@@ -184,12 +205,13 @@
     return pl.pallas_call(
         functools.partial(sweep_kernel, rows, cols),
         out_shape=jax.ShapeDtypeStruct((local_rows, rhs, width), jnp.float32),
-        in_specs=[vmem] * 4,
+        in_specs=[vmem] * (2 + 2 * local_cols),
         out_specs=vmem,
         scratch_shapes=[
             pltpu.VMEM((local_cols, rhs, width), jnp.float32),
             pltpu.VMEM((local_cols, rhs, width), jnp.float32),
             pltpu.VMEM((local_cols, rows - 1, rhs, width), jnp.float32),
+            pltpu.VMEM((local_cols, 4, width, width), jnp.bfloat16),
             dma((local_rows,)),
             dma((local_rows, cols)),
             dma((local_cols,)),
@@ -198,7 +220,7 @@
             dma((local_cols, rows - 1)),
         ],
         compiler_params=pltpu.CompilerParams(collective_id=0, has_side_effects=True),
-    )(tiles, inverse, below, target)
+    )(tiles, target, *inverses, *corrections)
 
 
 def body(factor_wide, factor_narrow, flags, forward_solution, solution_grad):
@@ -218,23 +240,29 @@
         return jnp.where(narrow, cut(factor_narrow).astype(jnp.float32), cut(factor_wide))
 
     targets = [my_col + col_count * s for s in range(local_cols)]
-    below = jnp.stack([
-        pick(jnp.minimum(j + 1, tile_count - 1) // row_count, s) for s, j in enumerate(targets)
-    ])
-    below = lax.ppermute(below, "row", [(i, (i - 1) % row_count) for i in range(row_count)])
+    holders = [
+        (r, c) for r in range(row_count) for c in range(col_count)
+        if any((c + col_count * s) % row_count == r for s in range(local_cols))
+    ]
+    to_holders = [
+        ((r + 1) % row_count * col_count + c, r * col_count + c) for r, c in holders
+    ]
+    below = [None] * local_cols
+    for s in reversed(range(local_cols)):
+        tile = pick(jnp.minimum(targets[s] + 1, tile_count - 1) // row_count, s)
+        below[s] = lax.ppermute(tile, ("row", "col"), to_holders)
     factor_tiles = jnp.where(
         flags[:, 0, :, 0, None, None] == 1,
         factor_narrow[:, 0, :, 0].astype(jnp.float32),
         factor_wide[:, 0, :, 0],
     )
-    diagonal = jnp.stack([pick(j // row_count, s) for s, j in enumerate(targets)])
-    inverse = invert(diagonal)
-    correction = jnp.einsum(
-        "sab,sbc->sac", below, inverse, precision=HIGHEST_PRECISION,
-        preferred_element_type=jnp.float32,
-    )
+    inverses = [invert(pick(j // row_count, s)) for s, j in enumerate(targets)]
+    corrections = [
+        jnp.dot(b, v, precision=PRODUCT_PRECISION, preferred_element_type=jnp.float32)
+        for b, v in zip(below, inverses)
+    ]
     target = jnp.swapaxes(solution_grad[:, 0], 1, 2)
-    solved = sweep(row_count, col_count, factor_tiles, inverse, correction, target)
+    solved = sweep(row_count, col_count, factor_tiles, target, inverses, corrections)
     row_index = jnp.arange(local_rows, dtype=jnp.int32) * row_count + my_row
     col_index = jnp.arange(local_cols, dtype=jnp.int32) * col_count + my_col
     products = -jnp.einsum(

time: 208 us -> 192 us (0.923)
  waiting for transfers between devices: 20.9 us -> 0.01 us
  Pallas kernels: 140 us -> 146 us
  matrix products: 13.5 us -> 16.6 us
  starting transfers between devices: 5.08 us -> 2.74 us
    ppermute x1 -> x2, waiting for transfers between devices: 20.9 us -> 0.01 us  [body(): below[s] = lax.ppermute(tile, ('row', 'col'), to_holders)]
    another operation x2 -> x0, other arithmetic: 2.97 us -> none  [the longest x1 1.49 us: body(): jnp.stack([pick(j // row_count, s) for s, j in enumerate(targets)])]
    pallas_call x1, Pallas kernels: 129 us -> 132 us  [sweep(): pl.pallas_call(functools.partial(sweep_kernel, rows, cols), out_shape=jax...]
    select_n x1 -> x2, other arithmetic: 0.82 us -> 3.33 us  [pick(): jnp.where(narrow, cut(factor_narrow).astype(jnp.float32), cut(factor_wide))]
    ppermute x1 -> x2, starting transfers between devices: 5.08 us -> 2.74 us  [body(): below[s] = lax.ppermute(tile, ('row', 'col'), to_holders)]
    pallas_call x1 -> x2, Pallas kernels: 11.8 us -> 13.9 us  [invert(): pl.pallas_call(invert_kernel, out_shape=jax.ShapeDtypeStruct(tile.shape,...]
    dot_general x1 -> x2, matrix products: 4.82 us -> 6.66 us  [body(): jnp.dot(b, v, precision=PRODUCT_PRECISION, preferred_element_type=jnp.flo...]
  transfers between devices with their start and end apart: 1 -> 2, of which waited for: 1 -> 0; matrix products, arithmetic and copies ran while one was open for 6% -> 8% of each run, Pallas kernels for 6% -> 7%
where the time goes in v2:
time: 192 us
  Pallas kernels  146 us (76%)
  matrix products  16.6 us (9%)
  other arithmetic  13.3 us (7%)
  local copies, waits for them, and re-layouts  10.2 us (5%)
  between operations  3.34 us (2%)
  starting transfers between devices  2.74 us (1%)
    pallas_call x1, Pallas kernels, sweep(): pl.pallas_call(functools.partial(sweep_kernel, rows, cols), out_shape=jax...  132 us
    pallas_call x2, Pallas kernels, invert(): pl.pallas_call(invert_kernel, out_shape=jax.ShapeDtypeStruct(tile.shape,...  13.9 us
    dot_general x1, matrix products, body(): jnp.einsum('ark,blr->abkl', solved, forward_solution[:, 0], precision=PRO...  9.91 us
    select_n x1, other arithmetic, body(): jnp.where(flags[:, 0, :, 0, None, None] == 1, factor_narrow[:, 0, :, 0].a...  9.76 us
    dot_general x2, matrix products, body(): jnp.dot(b, v, precision=PRODUCT_PRECISION, preferred_element_type=jnp.flo...  6.66 us
    slice x3, local copies, waits for them, and re-layouts, cut(): pool[:, 0, col_slot, 0]  5.86 us
  transfers between devices with their start and end apart: 2, of which 0 were waited for; matrix products, arithmetic and copies ran while one was open for 8% of the time, Pallas kernels for 7%

profile of v2, /device:TPU:0, one launch (start us, length us, event | category | flops | bytes accessed | tf_op | source)
XLA Modules:
  0.0 191.7 jit_solution(9182023918760422102)
XLA Ops:
  0.6 0.0 copy-start
  0.7 0.7 fusion.5
  1.4 0.7 constant_dynamic-slice_fusion
  3.3 0.0 copy-start.1
  3.3 4.7 %fusion.3 = (f32[4,1,1,1,512,512]{5,4,3,2,1,0:T(8,128)S(1)}, f32[4,1,1,1,512,512]{5,4,3,2,1,0:T(8,128)S(1)}) fusion(f32[4,1,2,1,512,512]{5,4,3,2,1,0:T(8,128)} %param.5), kind=kLoop, calls=%fused_computation.19 | loop fusion | bytes 16777216 | tf_op jit(solution)/shard_map/slice | solution.py:238
  8.0 0.0 copy-done.1
  8.0 0.5 fusion.4
  8.5 0.0 copy-start.5
  8.5 1.7 select_bitcast_fusion
  10.2 1.3 collective-permute-start.1
  12.8 0.0 copy-start.4
  12.8 1.7 select_bitcast_fusion.1
  14.4 1.5 collective-permute-start
  15.9 0.0 copy-done.5
  15.9 0.1 iota_compare_fusion
  16.0 7.0 %shard_map.69.refs_1_ = f32[512,512]{1,0:T(8,128)} custom-call(f32[512,512]{1,0:T(8,128)} %get-tuple-element.7.tile_ref), custom_call_target="tpu_custom_call" | custom-call | tf_op jit(solution)/shard_map/pallas_call | solution.py:67
  23.0 6.9 %shard_map.68.refs_0_ = f32[512,512]{1,0:T(8,128)} custom-call(f32[512,512]{1,0:T(8,128)} %get-tuple-element.9.tile_ref), custom_call_target="tpu_custom_call" | custom-call | tf_op jit(solution)/shard_map/pallas_call | solution.py:67
  29.9 0.1 copy.7
  30.0 0.0 copy-done.4
  30.0 1.0 copy.9
  31.1 0.1 broadcast_compare_fusion.1
  31.1 0.0 copy-start.2
  31.1 0.0 copy-start.3
  31.1 9.8 %convert_select_fusion.tiles_ref = f32[4,2,512,512]{3,2,1,0:T(8,128)} fusion(f32[4,1,2,1,512,512]{5,4,3,2,1,0:T(8,128)} %param.5, bf16[4,1,2,1,512,512]{5,4,3,2,1,0:T(8,128)(2,1)} %param.6, pred[4,2]{1,0:T(4,128)(4,1)S(1)} %bitcast.49), kind=kLoop, calls=%fused_computation | loop fusion | flops 4194304 | bytes 20971528 | tf_op jit(solution)/shard_map/jit(_where)/select_n | solution.py:254
  40.9 0.0 collective-permute-done.1
  40.9 0.0 copy-done.2
  40.9 3.2 %fusion.7.refs_3_ = f32[512,512]{1,0:T(8,128)} fusion(f32[512,512]{1,0:T(8,128)} %collective-permute-done.1, f32[512,512]{1,0:T(8,128)S(1)} %copy-done.2), kind=kOutput, calls=%fused_computation.23 | convolution fusion | flops 805306368 | bytes 3145728 | tf_op jit(solution)/shard_map/dot_general | solution.py:261
  44.1 0.0 collective-permute-done
  44.1 0.0 copy-done.3
  44.1 3.4 %fusion.6.refs_2_ = f32[512,512]{1,0:T(8,128)} fusion(f32[512,512]{1,0:T(8,128)} %collective-permute-done, f32[512,512]{1,0:T(8,128)S(1)} %copy-done.3), kind=kOutput, calls=%fused_computation.22 | convolution fusion | flops 805306368 | bytes 3145728 | tf_op jit(solution)/shard_map/dot_general | solution.py:261
  47.6 131.6 %shard_map.70 = f32[4,128,512]{2,1,0:T(8,128)} custom-call(f32[4,2,512,512]{3,2,1,0:T(8,128)} %convert_select_fusion.tiles_ref, f32[2,128,512]{2,1,0:T(8,128)} %bitcast.48, f32[512,512]{1,0:T(8,128)} %shard_map.68.refs_0_, f32[512,512]{1,0:T(8,128)} %shard_map.69.refs_1_, f32[512,512]{1,0:T(8,128)} %fusion.6.refs_2_, f32[512,512]{1,0:T(8,128)} %fusion.7.refs_3_), custom_call_target="tpu_custom_call" | custom-call | tf_op jit(solution)/shard_map/pallas_call | solution.py:205
  179.2 2.5 %copy.11 = f32[4,1,512,128]{3,2,1,0:T(8,128)} copy(f32[4,1,512,128]{2,3,0,1:T(8,128)} %bitcast.47) | data formatting | bytes 2097152
  181.7 0.0 copy-done
  181.7 9.9 %fusion = f32[4,1,2,1,512,512]{5,4,3,2,1,0:T(8,128)} fusion(pred[512,512]{1,0:T(8,128)(4,1)S(1)} %iota_compare_fusion, pred[4,2]{1,0:T(4,128)(4,1)S(1)} %get-tuple-element.13, pred[4,2]{1,0:T(4,128)(4,1)S(1)} %get-tuple-element.12, f32[4,128,512]{2,1,0:T(8,128)} %shard_map.70, f32[2,1,512,128]{3,2,1,0:T(8,128)S(1)} %copy-done), kind=kOutput, calls=%fused_computation.2 | convolution fusion | flops 1619001344 | bytes 10223632 | tf_op jit(solution)/shard_map/ark,blr->abkl/dot_general | solution.py:268
  (3 shorter events, 0.0 us)
Async XLA Ops:
  0.6 181.1 %copy-start = (f32[2,1,512,128]{3,2,1,0:T(8,128)S(1)}, f32[2,1,512,128]{3,2,1,0:T(8,128)}, u32[]{:S(2)}) copy-start(f32[2,1,512,128]{3,2,1,0:T(8,128)} %param.8) | copy-start | bytes 1572868
  3.3 4.7 %copy-start.1 = (bf16[4,1,2,1,512,512]{5,4,3,2,1,0:T(8,128)(2,1)S(1)}, bf16[4,1,2,1,512,512]{5,4,3,2,1,0:T(8,128)(2,1)}, u32[]{:S(2)}) copy-start(bf16[4,1,2,1,512,512]{5,4,3,2,1,0:T(8,128)(2,1)} %param.6) | copy-start | bytes 12582916
  8.5 7.4 %copy-start.5 = (s32[4,1,2,1]{0,3,2,1:T(1,128)S(1)}, s32[4,1,2,1]{0,3,2,1:T(1,128)}, u32[]{:S(2)}) copy-start(s32[4,1,2,1]{0,3,2,1:T(1,128)} %param.7) | copy-start | bytes 100
  10.2 30.7 %collective-permute-start.1 = (f32[512,512]{1,0:T(8,128)}, f32[512,512]{1,0:T(8,128)}, u32[]{:S(2)}, u32[]{:S(2)}) collective-permute-start(f32[512,512]{1,0:T(8,128)} %get-tuple-element.6), channel_id=1, source_target_pairs={{8,0},{12,4},{17,9},{21,13},{26,18},{30,22},{3,27},{7,31}} | collective-permute-start | bytes 3145736 | tf_op jit(solution)/shard_map/ppermute | solution.py:253
  12.8 17.3 %copy-start.4 = (f32[2,1,512,128]{3,2,1,0:T(8,128)S(1)}, f32[2,1,512,128]{3,2,1,0:T(8,128)}, u32[]{:S(2)}) copy-start(f32[2,1,512,128]{3,2,1,0:T(8,128)} %param.9) | copy-start | bytes 1572868
  14.4 29.7 %collective-permute-start = (f32[512,512]{1,0:T(8,128)}, f32[512,512]{1,0:T(8,128)}, u32[]{:S(2)}, u32[]{:S(2)}) collective-permute-start(f32[512,512]{1,0:T(8,128)} %get-tuple-element.8), channel_id=1, source_target_pairs={{8,0},{12,4},{17,9},{21,13},{26,18},{30,22},{3,27},{7,31}} | collective-permute-start | bytes 3145736 | tf_op jit(solution)/shard_map/ppermute | solution.py:253
  31.1 9.8 %copy-start.2 = (f32[512,512]{1,0:T(8,128)S(1)}, f32[512,512]{1,0:T(8,128)}, u32[]{:S(2)}) copy-start(f32[512,512]{1,0:T(8,128)} %shard_map.69.refs_1_) | copy-start | bytes 3145732
  31.1 13.0 %copy-start.3 = (f32[512,512]{1,0:T(8,128)S(1)}, f32[512,512]{1,0:T(8,128)}, u32[]{:S(2)}) copy-start(f32[512,512]{1,0:T(8,128)} %shard_map.68.refs_0_) | copy-start | bytes 3145732
